TPU v7x, 32 devices: a whole 2x2x4 slice. The times are simulated.
32 devices in a mesh: lat: 8 (over y, x, core), lon: 4 (over z).
Axes of the slice: x: 2, y: 2, z: 4, core: 2. Of those that a mesh axis runs over, the one named last changes fastest.
Arguments:
- inputs: bfloat16 [128, 384, 256], P('lat', 'lon'), may hold values from -6 to 6
- first_filter: bfloat16 [3, 3, 256, 256], replicated, may hold values from -0.125 to 0.125
- second_filter: bfloat16 [3, 3, 256, 256], replicated, may hold values from -0.125 to 0.125
- cotangent: bfloat16 [128, 384, 256], P('lat', 'lon'), may hold values from -30 to 30
Outputs:
- input_grad: bfloat16 [128, 384, 256], P('lat', 'lon')
- first_grad: float32 [3, 3, 256, 256], replicated
- second_grad: float32 [3, 3, 256, 256], replicated
All inputs are finite; a program needn't handle non-finite values.
Results may differ from a plain program's by a relative error of at most 0.0061.
Values may be sent and summed in bfloat16 or wider, within the bound.
A program may use at most 64 MiB of HBM per device.

v0:
```python
import jax
import jax.numpy as jnp
from jax import lax
from jax.sharding import PartitionSpec as P


def extended(block, sides, width):
    for axis, dim in sides:
        count = lax.axis_size(axis)
        forward = [(i, i + 1) for i in range(count - 1)]
        forward.append((count - 1, 0))
        backward = [(target, source) for source, target in forward]
        low = lax.ppermute(
            lax.slice_in_dim(block, block.shape[dim] - width, None, axis=dim), axis, forward
        )
        high = lax.ppermute(lax.slice_in_dim(block, 0, width, axis=dim), axis, backward)
        block = jnp.concatenate([low, block, high], axis=dim)
    return block


def mask_rows(padded, width):
    rows = padded.shape[0] - 2 * width
    position = lax.broadcasted_iota(jnp.int32, (padded.shape[0], 1, 1), 0)
    index = lax.axis_index("lat")
    count = lax.axis_size("lat")
    dropped = (position < width) & (index == 0) | (position >= rows + width) & (index == count - 1)
    return jnp.where(dropped, jnp.zeros((), padded.dtype), padded)


def extend(field):
    padded = extended(field, (("lat", 0), ("lon", 1)), 1)
    return mask_rows(padded, 1)


def conv_taps(padded, weight, rows, cols, flipped):
    total = jnp.zeros(
        (rows * cols, weight.shape[3] if not flipped else weight.shape[2]), jnp.float32
    )
    for first in range(3):
        for second in range(3):
            piece = padded[first : first + rows, second : second + cols, :].reshape(rows * cols, -1)
            if flipped:
                total = total + lax.dot_general(
                    piece,
                    weight[2 - first, 2 - second],
                    (((1,), (1,)), ((), ())),
                    preferred_element_type=jnp.float32,
                )
            else:
                total = total + jnp.dot(
                    piece, weight[first, second], preferred_element_type=jnp.float32
                )
    return total.reshape(rows, cols, -1)


def filter_grad(padded, delta, rows, cols):
    flat = delta.reshape(rows * cols, -1)
    taps = []
    for first in range(3):
        for second in range(3):
            piece = padded[first : first + rows, second : second + cols, :].reshape(rows * cols, -1)
            taps.append(
                lax.dot_general(
                    piece, flat, (((0,), (0,)), ((), ())), preferred_element_type=jnp.float32
                )
            )
    return jnp.stack(taps).reshape(3, 3, flat.shape[1], flat.shape[1])


def gelu_value(value):
    return value * 0.5 * (1.0 + jax.scipy.special.erf(value * 0.7071067811865476))


def gelu_slope(value):
    return (
        0.5 * (1.0 + jax.scipy.special.erf(value * 0.7071067811865476))
        + value * jnp.exp(-0.5 * value * value) * 0.3989422804014327
    )


def body(inputs, first_filter, second_filter, cotangent):
    rows, cols = (inputs.shape[0], inputs.shape[1])
    padded_in = extend(inputs)
    hidden_one = conv_taps(padded_in, first_filter, rows, cols, False)
    act = gelu_value(hidden_one).astype(jnp.bfloat16)
    padded_act = extend(act)
    hidden_two = conv_taps(padded_act, second_filter, rows, cols, False)
    delta_two = (cotangent.astype(jnp.float32) * gelu_slope(hidden_two)).astype(jnp.bfloat16)
    second_part = filter_grad(padded_act, delta_two, rows, cols)
    act_grad = conv_taps(extend(delta_two), second_filter, rows, cols, True)
    delta_one = (act_grad * gelu_slope(hidden_one)).astype(jnp.bfloat16)
    first_part = filter_grad(padded_in, delta_one, rows, cols)
    first_grad, second_grad = lax.psum((first_part, second_part), ("lat", "lon"))
    input_grad = conv_taps(extend(delta_one), first_filter, rows, cols, True).astype(jnp.bfloat16)
    return (input_grad, first_grad, second_grad)


def solution(mesh):
    in_specs = (P("lat", "lon", None), P(), P(), P("lat", "lon", None))
    out_specs = (P("lat", "lon", None), P(), P())
    return jax.shard_map(body, mesh=mesh, in_specs=in_specs, out_specs=out_specs, check_vma=False)
```

profile of v0, /device:TPU:0, one launch (start us, length us, event | category | flops | bytes accessed | tf_op | source)
XLA Modules:
  0.0 228.8 jit_solution(7460417335077282387)
XLA Ops:
  7.2 0.8 fusion.133
  8.0 0.5 collective-permute-start
  8.6 2.9 %collective-permute-start.1 = (bf16[1,96,256]{2,1,0:T(8,128)(2,1)S(1)}, bf16[1,96,256]{2,1,0:T(8,128)(2,1)S(1)}, u32[]{:S(2)}, u32[]{:S(2)}) collective-permute-start(bf16[1,96,256]{2,1,0:T(8,128)(2,1)S(1)} %get-tuple-element.55), channel_id=1, source_target_pairs={{4,0},{8,4},{12,8},{16,12},{20,16},{24,20},{28,24},{0,28},{5,1},{9... | collective-permute-start | bytes 147464 | tf_op jit(solution)/shard_map/ppermute | solution.py:16
  11.5 1.7 collective-permute-done
  13.2 1.2 constant_dynamic-update-slice_fusion.1
  14.5 4.4 %collective-permute-start.3 = (bf16[18,1,256]{2,1,0:T(2,128)(2,1)S(1)}, bf16[18,1,256]{2,1,0:T(2,128)(2,1)S(1)}, u32[]{:S(2)}, u32[]{:S(2)}) collective-permute-start(bf16[18,1,256]{2,1,0:T(2,128)(2,1)S(1)} %get-tuple-element.48), channel_id=1, source_target_pairs={{1,0},{2,1},{3,2},{0,3},{5,4},{6,5},{7,6},{4,7},{9,8},{10,9},{11,1... | collective-permute-start | bytes 27656 | tf_op jit(solution)/shard_map/ppermute | solution.py:16
  18.9 1.5 collective-permute-done.3
  20.3 4.1 %collective-permute-done.2 = bf16[18,1,256]{2,1,0:T(2,128)(2,1)S(1)} collective-permute-done((bf16[18,1,256]{2,1,0:T(2,128)(2,1)S(1)}, bf16[18,1,256]{2,1,0:T(2,128)(2,1)S(1)}, u32[]{:S(2)}, u32[]{:S(2)}) %collective-permute-start.2) | collective-permute-done | bytes 9248 | tf_op jit(solution)/shard_map/ppermute | solution.py:13
  24.4 0.6 maximum_select_fusion
  25.0 0.8 fusion.128
  25.9 0.4 copy-done.1
  30.0 0.5 collective-permute-start.4
  30.5 1.4 collective-permute-done.5
  31.9 2.6 %collective-permute-done.4 = bf16[1,96,256]{2,1,0:T(8,128)(2,1)S(1)} collective-permute-done((bf16[1,96,256]{2,1,0:T(8,128)(2,1)S(1)}, bf16[1,96,256]{2,1,0:T(8,128)(2,1)S(1)}, u32[]{:S(2)}, u32[]{:S(2)}) %collective-permute-start.4) | collective-permute-done | bytes 49184 | tf_op jit(solution)/shard_map/ppermute | solution.py:13
  34.8 1.8 collective-permute-start.6
  36.6 1.7 collective-permute-done.7
  38.4 2.0 collective-permute-done.6
  40.4 0.6 maximum_select_fusion.1
  40.9 1.1 fusion.127
  45.5 0.7 copy-done.5
  46.3 0.7 fusion.6
  47.0 0.4 fusion.21
  47.5 0.5 collective-permute-start.8
  48.0 0.4 fusion.20
  48.4 0.4 fusion.19
  48.8 0.4 fusion.18
  49.3 0.4 fusion.17
  49.7 0.4 fusion.16
  50.1 0.4 fusion.15
  50.5 0.4 fusion.14
  51.0 1.1 collective-permute-done.8
  52.2 2.0 collective-permute-start.10
  54.2 0.4 fusion.13
  54.7 1.3 collective-permute-done.11
  56.0 1.9 collective-permute-done.10
  57.8 0.6 maximum_select_fusion.2
  58.4 1.1 fusion.126
  63.1 0.7 fusion.12
  64.2 0.6 collective-permute-start.13
  64.8 0.4 fusion.29
  65.2 0.4 fusion.28
  65.7 0.4 fusion.27
  66.1 0.4 fusion.26
  66.5 0.4 fusion.25
  66.9 0.4 fusion.24
  67.4 0.4 fusion.23
  67.8 1.4 collective-permute-done.12
  69.3 2.0 collective-permute-start.14
  71.3 0.4 fusion.22
  71.8 1.4 copy-done.4
  73.2 2.0 collective-permute-done.14
  75.1 0.6 maximum_select_fusion.3
  75.7 1.1 fusion.125
  77.2 0.4 convolution_add_fusion.7
  77.6 0.4 convolution_add_fusion.6
  78.0 0.4 convolution_add_fusion.5
  78.4 0.4 convolution_add_fusion.4
  78.9 0.4 convolution_add_fusion.3
  79.3 0.4 convolution_add_fusion.2
  79.7 0.4 convolution_add_fusion.1
  80.1 1.3 fusion
  81.4 135.8 %all-reduce.3.cloned.1.call-done = (f32[3,3,256,256]{3,2,1,0:T(8,128)}, f32[3,3,256,256]{3,2,1,0:T(8,128)}) async-done(((f32[3,3,256,256]{3,2,1,0:T(8,128)}, f32[3,3,256,256]{3,2,1,0:T(8,128)}), (f32[3,3,256,256]{3,2,1,0:T(8,128)}, f32[3,3,256,256]{3,2,1,0:T(8,128)})) %all-reduce.3.cloned.1.call-update) | async-done | bytes 4718608 | tf_op jit(solution)/shard_map/psum | solution.py:93
  217.2 3.4 %copy.27 = f32[3,3,256,256]{3,2,1,0:T(8,128)} copy(f32[3,3,256,256]{3,2,1,0:T(8,128)} %get-tuple-element.58) | data formatting | bytes 4718592
  220.5 1.4 copy.28
  (62 shorter events, 12.2 us)
Async XLA Ops:
  7.2 210.0 %all-reduce.3.cloned.1.call-start = ((), (), s32[]{:S(2)}) async-start(), calls=%async_computation | async-start | bytes 9437184 | tf_op jit(solution)/shard_map/psum | solution.py:93
  8.0 5.2 %collective-permute-start = (bf16[1,96,256]{2,1,0:T(8,128)(2,1)S(1)}, bf16[1,96,256]{2,1,0:T(8,128)(2,1)S(1)}, u32[]{:S(2)}, u32[]{:S(2)}) collective-permute-start(bf16[1,96,256]{2,1,0:T(8,128)(2,1)S(1)} %get-tuple-element.56), channel_id=1, source_target_pairs={{0,4},{4,8},{8,12},{12,16},{16,20},{20,24},{24,28},{28,0},{1,5},{5... | collective-permute-start | bytes 147464 | tf_op jit(solution)/shard_map/ppermute | solution.py:13
  8.6 5.8 %collective-permute-start.1 = (bf16[1,96,256]{2,1,0:T(8,128)(2,1)S(1)}, bf16[1,96,256]{2,1,0:T(8,128)(2,1)S(1)}, u32[]{:S(2)}, u32[]{:S(2)}) collective-permute-start(bf16[1,96,256]{2,1,0:T(8,128)(2,1)S(1)} %get-tuple-element.55), channel_id=1, source_target_pairs={{4,0},{8,4},{12,8},{16,12},{20,16},{24,20},{28,24},{0,28},{5,1},{9... | collective-permute-start | bytes 147464 | tf_op jit(solution)/shard_map/ppermute | solution.py:16
  14.5 5.9 %collective-permute-start.3 = (bf16[18,1,256]{2,1,0:T(2,128)(2,1)S(1)}, bf16[18,1,256]{2,1,0:T(2,128)(2,1)S(1)}, u32[]{:S(2)}, u32[]{:S(2)}) collective-permute-start(bf16[18,1,256]{2,1,0:T(2,128)(2,1)S(1)} %get-tuple-element.48), channel_id=1, source_target_pairs={{1,0},{2,1},{3,2},{0,3},{5,4},{6,5},{7,6},{4,7},{9,8},{10,9},{11,1... | collective-permute-start | bytes 27656 | tf_op jit(solution)/shard_map/ppermute | solution.py:16
  18.9 5.6 %collective-permute-start.2 = (bf16[18,1,256]{2,1,0:T(2,128)(2,1)S(1)}, bf16[18,1,256]{2,1,0:T(2,128)(2,1)S(1)}, u32[]{:S(2)}, u32[]{:S(2)}) collective-permute-start(bf16[18,1,256]{2,1,0:T(2,128)(2,1)S(1)} %get-tuple-element.47), channel_id=1, source_target_pairs={{0,1},{1,2},{2,3},{3,0},{4,5},{5,6},{6,7},{7,4},{8,9},{9,10},{10,1... | collective-permute-start | bytes 27656 | tf_op jit(solution)/shard_map/ppermute | solution.py:13
  25.0 1.3 copy-start.1
  30.0 2.0 collective-permute-start.5
  30.0 4.5 %collective-permute-start.4 = (bf16[1,96,256]{2,1,0:T(8,128)(2,1)S(1)}, bf16[1,96,256]{2,1,0:T(8,128)(2,1)S(1)}, u32[]{:S(2)}, u32[]{:S(2)}) collective-permute-start(bf16[1,96,256]{2,1,0:T(8,128)(2,1)S(1)} %get-tuple-element.53), channel_id=1, source_target_pairs={{0,4},{4,8},{8,12},{12,16},{16,20},{20,24},{24,28},{28,0},{1,5},{5... | collective-permute-start | bytes 147464 | tf_op jit(solution)/shard_map/ppermute | solution.py:13
  34.5 3.8 %collective-permute-start.7 = (bf16[18,1,256]{2,1,0:T(2,128)(2,1)S(1)}, bf16[18,1,256]{2,1,0:T(2,128)(2,1)S(1)}, u32[]{:S(2)}, u32[]{:S(2)}) collective-permute-start(bf16[18,1,256]{2,1,0:T(2,128)(2,1)S(1)} %get-tuple-element.46), channel_id=1, source_target_pairs={{1,0},{2,1},{3,2},{0,3},{5,4},{6,5},{7,6},{4,7},{9,8},{10,9},{11,1... | collective-permute-start | bytes 27656 | tf_op jit(solution)/shard_map/ppermute | solution.py:16
  34.8 5.6 %collective-permute-start.6 = (bf16[18,1,256]{2,1,0:T(2,128)(2,1)S(1)}, bf16[18,1,256]{2,1,0:T(2,128)(2,1)S(1)}, u32[]{:S(2)}, u32[]{:S(2)}) collective-permute-start(bf16[18,1,256]{2,1,0:T(2,128)(2,1)S(1)} %get-tuple-element.45), channel_id=1, source_target_pairs={{0,1},{1,2},{2,3},{3,0},{4,5},{5,6},{6,7},{7,4},{8,9},{9,10},{10,1... | collective-permute-start | bytes 27656 | tf_op jit(solution)/shard_map/ppermute | solution.py:13
  40.9 1.3 copy-start
  45.1 1.1 copy-start.5
  47.4 3.6 %collective-permute-start.9 = (bf16[1,96,256]{2,1,0:T(8,128)(2,1)S(1)}, bf16[1,96,256]{2,1,0:T(8,128)(2,1)S(1)}, u32[]{:S(2)}, u32[]{:S(2)}) collective-permute-start(bf16[1,96,256]{2,1,0:T(8,128)(2,1)S(1)} %get-tuple-element.52), channel_id=1, source_target_pairs={{4,0},{8,4},{12,8},{16,12},{20,16},{24,20},{28,24},{0,28},{5,1},{9... | collective-permute-start | bytes 147464 | tf_op jit(solution)/shard_map/ppermute | solution.py:16
  47.5 4.6 %collective-permute-start.8 = (bf16[1,96,256]{2,1,0:T(8,128)(2,1)S(1)}, bf16[1,96,256]{2,1,0:T(8,128)(2,1)S(1)}, u32[]{:S(2)}, u32[]{:S(2)}) collective-permute-start(bf16[1,96,256]{2,1,0:T(8,128)(2,1)S(1)} %get-tuple-element.51), channel_id=1, source_target_pairs={{0,4},{4,8},{8,12},{12,16},{16,20},{20,24},{24,28},{28,0},{1,5},{5... | collective-permute-start | bytes 147464 | tf_op jit(solution)/shard_map/ppermute | solution.py:13
  52.2 3.8 %collective-permute-start.11 = (bf16[18,1,256]{2,1,0:T(2,128)(2,1)S(1)}, bf16[18,1,256]{2,1,0:T(2,128)(2,1)S(1)}, u32[]{:S(2)}, u32[]{:S(2)}) collective-permute-start(bf16[18,1,256]{2,1,0:T(2,128)(2,1)S(1)} %get-tuple-element.44), channel_id=1, source_target_pairs={{1,0},{2,1},{3,2},{0,3},{5,4},{6,5},{7,6},{4,7},{9,8},{10,9},{11,1... | collective-permute-start | bytes 27656 | tf_op jit(solution)/shard_map/ppermute | solution.py:16
  52.2 5.6 %collective-permute-start.10 = (bf16[18,1,256]{2,1,0:T(2,128)(2,1)S(1)}, bf16[18,1,256]{2,1,0:T(2,128)(2,1)S(1)}, u32[]{:S(2)}, u32[]{:S(2)}) collective-permute-start(bf16[18,1,256]{2,1,0:T(2,128)(2,1)S(1)} %get-tuple-element.43), channel_id=1, source_target_pairs={{0,1},{1,2},{2,3},{3,0},{4,5},{5,6},{6,7},{7,4},{8,9},{9,10},{10,1... | collective-permute-start | bytes 27656 | tf_op jit(solution)/shard_map/ppermute | solution.py:13
  54.7 4.8 %copy-start.3 = (f32[9,256,256]{2,1,0:T(8,128)}, f32[9,256,256]{2,1,0:T(8,128)S(1)}, u32[]{:S(2)}) copy-start(f32[9,256,256]{2,1,0:T(8,128)S(1)} %fusion.13) | copy-start | bytes 7077892
  64.2 3.6 %collective-permute-start.13 = (bf16[1,96,256]{2,1,0:T(8,128)(2,1)S(1)}, bf16[1,96,256]{2,1,0:T(8,128)(2,1)S(1)}, u32[]{:S(2)}, u32[]{:S(2)}) collective-permute-start(bf16[1,96,256]{2,1,0:T(8,128)(2,1)S(1)} %get-tuple-element.50), channel_id=1, source_target_pairs={{4,0},{8,4},{12,8},{16,12},{20,16},{24,20},{28,24},{0,28},{5,1},{9... | collective-permute-start | bytes 147464 | tf_op jit(solution)/shard_map/ppermute | solution.py:16
  64.8 4.4 %collective-permute-start.12 = (bf16[1,96,256]{2,1,0:T(8,128)(2,1)S(1)}, bf16[1,96,256]{2,1,0:T(8,128)(2,1)S(1)}, u32[]{:S(2)}, u32[]{:S(2)}) collective-permute-start(bf16[1,96,256]{2,1,0:T(8,128)(2,1)S(1)} %get-tuple-element.49), channel_id=1, source_target_pairs={{0,4},{4,8},{8,12},{12,16},{16,20},{20,24},{24,28},{28,0},{1,5},{5... | collective-permute-start | bytes 147464 | tf_op jit(solution)/shard_map/ppermute | solution.py:13
  69.2 3.9 %collective-permute-start.15 = (bf16[18,1,256]{2,1,0:T(2,128)(2,1)S(1)}, bf16[18,1,256]{2,1,0:T(2,128)(2,1)S(1)}, u32[]{:S(2)}, u32[]{:S(2)}) collective-permute-start(bf16[18,1,256]{2,1,0:T(2,128)(2,1)S(1)} %get-tuple-element.42), channel_id=1, source_target_pairs={{1,0},{2,1},{3,2},{0,3},{5,4},{6,5},{7,6},{4,7},{9,8},{10,9},{11,1... | collective-permute-start | bytes 27656 | tf_op jit(solution)/shard_map/ppermute | solution.py:16
  69.3 5.8 %collective-permute-start.14 = (bf16[18,1,256]{2,1,0:T(2,128)(2,1)S(1)}, bf16[18,1,256]{2,1,0:T(2,128)(2,1)S(1)}, u32[]{:S(2)}, u32[]{:S(2)}) collective-permute-start(bf16[18,1,256]{2,1,0:T(2,128)(2,1)S(1)} %get-tuple-element.41), channel_id=1, source_target_pairs={{0,1},{1,2},{2,3},{3,0},{4,5},{5,6},{6,7},{7,4},{8,9},{9,10},{10,1... | collective-permute-start | bytes 27656 | tf_op jit(solution)/shard_map/ppermute | solution.py:13
  71.7 1.4 copy-start.4
  217.2 3.4 %copy-start.2 = (f32[3,3,256,256]{3,2,1,0:T(8,128)S(1)}, f32[3,3,256,256]{3,2,1,0:T(8,128)}, u32[]{:S(2)}) copy-start(f32[3,3,256,256]{3,2,1,0:T(8,128)} %get-tuple-element.59) | copy-start | bytes 7077892
Sparse Core Ops, SparseCore 0:
  73.3 143.8 all-reduce.2
where the time goes:
time: 229 us
  waiting for transfers between devices  158 us (69%)
  matrix products  22.3 us (10%)
  starting transfers between devices  15.8 us (7%)
  between operations  14.6 us (6%)
  local copies, waits for them, and re-layouts  13.6 us (6%)
  other arithmetic  4.03 us (2%)
    psum x1, waiting for transfers between devices, body(): lax.psum((first_part, second_part), ('lat', 'lon'))  136 us
    ppermute x8, waiting for transfers between devices, extended(): lax.ppermute(lax.slice_in_dim(block, block.shape[dim] - width, None, axis...  16.7 us
    unnamed x16, local copies, waits for them, and re-layouts  8.77 us
    ppermute x8, starting transfers between devices, extended(): lax.ppermute(lax.slice_in_dim(block, 0, width, axis=dim), axis, backward)  8.4 us
    dot_general x18, matrix products, conv_taps(): lax.dot_general(piece, weight[2 - first, 2 - second], (((1,), (1,)), ((),...  8.18 us
    dot_general x18, matrix products, filter_grad(): lax.dot_general(piece, flat, (((0,), (0,)), ((), ())), preferred_element_...  7.54 us
    ppermute x8, starting transfers between devices, extended(): lax.ppermute(lax.slice_in_dim(block, block.shape[dim] - width, None, axis...  7.38 us
    dot_general x18, matrix products, conv_taps(): jnp.dot(piece, weight[first, second], preferred_element_type=jnp.float32)  6.59 us
  transfers between devices with their start and end apart: 17, of which 13 were waited for; matrix products, arithmetic and copies ran while one was open for 6% of the time, Pallas kernels for 0%

commit v1 on v0

--- a/solution.py
+++ b/solution.py
@@ -2,6 +2,12 @@
 import jax.numpy as jnp
 from jax import lax
 from jax.sharding import PartitionSpec as P
+
+
+def zone_lead(z_in):
+    for nth in ("lat", "lon"):
+        z_in = lax.psum(z_in, nth)
+    return z_in
 
 
 def extended(block, sides, width):
@@ -90,7 +96,7 @@
     act_grad = conv_taps(extend(delta_two), second_filter, rows, cols, True)
     delta_one = (act_grad * gelu_slope(hidden_one)).astype(jnp.bfloat16)
     first_part = filter_grad(padded_in, delta_one, rows, cols)
-    first_grad, second_grad = lax.psum((first_part, second_part), ("lat", "lon"))
+    first_grad, second_grad = zone_lead((first_part, second_part))
     input_grad = conv_taps(extend(delta_one), first_filter, rows, cols, True).astype(jnp.bfloat16)
     return (input_grad, first_grad, second_grad)
 

time: 229 us -> 340 us (1.48)
  waiting for transfers between devices: 158 us -> 267 us
    psum x1 -> x2, waiting for transfers between devices: 136 us -> 238 us  [zone_lead(): z_in = lax.psum(z_in, nth)]
    ppermute x8, waiting for transfers between devices: 5.89 us -> 9.75 us  [extended(): lax.ppermute(lax.slice_in_dim(block, 0, width, axis=dim), axis, backward)]
    ppermute x8, starting transfers between devices: 8.4 us -> 12.1 us  [extended(): lax.ppermute(lax.slice_in_dim(block, 0, width, axis=dim), axis, backward)]
  transfers between devices with their start and end apart: 17 -> 18, of which waited for: 13 -> 16; matrix products, arithmetic and copies ran while one was open for 6% -> 3% of each run, Pallas kernels for 0% -> 0%
where the time goes in v1:
time: 340 us
  waiting for transfers between devices  267 us (79%)
  matrix products  22.3 us (7%)
  starting transfers between devices  17.6 us (5%)
  between operations  14.6 us (4%)
  local copies, waits for them, and re-layouts  13.6 us (4%)
  other arithmetic  4.03 us (1%)
    psum x2, waiting for transfers between devices, zone_lead(): z_in = lax.psum(z_in, nth)  238 us
    ppermute x8, waiting for transfers between devices, extended(): lax.ppermute(lax.slice_in_dim(block, block.shape[dim] - width, None, axis...  20 us
    ppermute x8, starting transfers between devices, extended(): lax.ppermute(lax.slice_in_dim(block, 0, width, axis=dim), axis, backward)  12.1 us
    ppermute x8, waiting for transfers between devices, extended(): lax.ppermute(lax.slice_in_dim(block, 0, width, axis=dim), axis, backward)  9.75 us
    unnamed x16, local copies, waits for them, and re-layouts  8.77 us
    dot_general x18, matrix products, conv_taps(): lax.dot_general(piece, weight[2 - first, 2 - second], (((1,), (1,)), ((),...  8.18 us
    dot_general x18, matrix products, filter_grad(): lax.dot_general(piece, flat, (((0,), (0,)), ((), ())), preferred_element_...  7.53 us
  transfers between devices with their start and end apart: 18, of which 16 were waited for; matrix products, arithmetic and copies ran while one was open for 3% of the time, Pallas kernels for 0%

profile of v1, /device:TPU:0, one launch (start us, length us, event | category | flops | bytes accessed | tf_op | source)
XLA Modules:
  0.0 339.5 jit_solution(3851944277064034261)
XLA Ops:
  7.2 0.8 fusion.133
  8.0 0.5 collective-permute-start
  8.6 2.9 collective-permute-start.1
  11.5 1.7 collective-permute-done
  13.2 1.2 constant_dynamic-update-slice_fusion.1
  14.5 4.4 %collective-permute-start.3 = (bf16[18,1,256]{2,1,0:T(2,128)(2,1)S(1)}, bf16[18,1,256]{2,1,0:T(2,128)(2,1)S(1)}, u32[]{:S(2)}, u32[]{:S(2)}) collective-permute-start(bf16[18,1,256]{2,1,0:T(2,128)(2,1)S(1)} %get-tuple-element.50), channel_id=1, source_target_pairs={{1,0},{2,1},{3,2},{0,3},{5,4},{6,5},{7,6},{4,7},{9,8},{10,9},{11,1... | collective-permute-start | bytes 27656 | tf_op jit(solution)/shard_map/ppermute | solution.py:22
  18.9 1.5 collective-permute-done.3
  20.3 4.1 %collective-permute-done.2 = bf16[18,1,256]{2,1,0:T(2,128)(2,1)S(1)} collective-permute-done((bf16[18,1,256]{2,1,0:T(2,128)(2,1)S(1)}, bf16[18,1,256]{2,1,0:T(2,128)(2,1)S(1)}, u32[]{:S(2)}, u32[]{:S(2)}) %collective-permute-start.2) | collective-permute-done | bytes 9248 | tf_op jit(solution)/shard_map/ppermute | solution.py:19
  24.4 0.6 maximum_select_fusion
  25.0 0.8 fusion.128
  25.9 0.4 copy-done.1
  30.0 0.5 collective-permute-start.4
  30.5 1.4 collective-permute-done.5
  31.9 2.6 collective-permute-done.4
  34.8 1.8 collective-permute-start.6
  36.6 1.7 collective-permute-done.7
  38.4 2.0 collective-permute-done.6
  40.4 0.6 maximum_select_fusion.1
  40.9 1.1 fusion.127
  45.5 0.7 copy-done.5
  46.3 0.7 fusion.6
  47.5 0.5 collective-permute-start.8
  48.0 0.4 fusion.20
  48.4 0.4 fusion.19
  48.8 0.4 fusion.18
  49.3 0.4 fusion.17
  49.7 0.4 fusion.16
  50.1 0.4 fusion.15
  50.5 0.4 fusion.14
  51.0 1.1 collective-permute-done.8
  52.2 2.0 collective-permute-start.10
  54.2 0.4 fusion.13
  54.7 1.3 collective-permute-done.11
  56.0 1.9 collective-permute-done.10
  57.8 0.6 maximum_select_fusion.2
  58.4 1.1 fusion.126
  63.1 0.7 fusion.12
  64.2 0.4 fusion.29
  64.6 0.4 fusion.28
  65.5 0.4 fusion.26
  65.9 0.4 fusion.25
  66.3 0.4 fusion.24
  66.7 0.4 fusion.23
  67.2 0.4 fusion.22
  67.6 1.4 copy-done.4
  69.1 84.2 %all-reduce.5.cloned.1.call-done = (f32[3,3,256,256]{3,2,1,0:T(8,128)}, f32[3,3,256,256]{3,2,1,0:T(8,128)}) async-done(((f32[3,3,256,256]{3,2,1,0:T(8,128)}, f32[3,3,256,256]{3,2,1,0:T(8,128)}), (f32[3,3,256,256]{3,2,1,0:T(8,128)}, f32[3,3,256,256]{3,2,1,0:T(8,128)})) %all-reduce.5.cloned.1.call-update) | async-done | bytes 4718608 | tf_op jit(solution)/shard_map/psum | solution.py:9
  153.3 1.0 collective-permute-start.13
  154.3 2.1 collective-permute-done.13
  156.4 2.3 collective-permute-done.12
  158.7 3.4 collective-permute-start.15
  162.1 1.8 collective-permute-done.15
  163.9 4.3 %collective-permute-done.14 = bf16[18,1,256]{2,1,0:T(2,128)(2,1)S(1)} collective-permute-done((bf16[18,1,256]{2,1,0:T(2,128)(2,1)S(1)}, bf16[18,1,256]{2,1,0:T(2,128)(2,1)S(1)}, u32[]{:S(2)}, u32[]{:S(2)}) %collective-permute-start.14) | collective-permute-done | bytes 9248 | tf_op jit(solution)/shard_map/ppermute | solution.py:19
  168.2 0.6 maximum_select_fusion.3
  168.8 1.1 fusion.125
  170.3 0.4 convolution_add_fusion.7
  170.7 0.4 convolution_add_fusion.6
  171.1 0.4 convolution_add_fusion.5
  171.5 0.4 convolution_add_fusion.4
  171.9 0.4 convolution_add_fusion.3
  172.4 0.4 convolution_add_fusion.2
  173.2 1.3 fusion
  174.5 153.4 %all-reduce.7.cloned.1.call-done = (f32[3,3,256,256]{3,2,1,0:T(8,128)}, f32[3,3,256,256]{3,2,1,0:T(8,128)}) async-done(((f32[3,3,256,256]{3,2,1,0:T(8,128)}, f32[3,3,256,256]{3,2,1,0:T(8,128)}), (f32[3,3,256,256]{3,2,1,0:T(8,128)}, f32[3,3,256,256]{3,2,1,0:T(8,128)})) %all-reduce.7.cloned.1.call-update) | async-done | bytes 4718608 | tf_op jit(solution)/shard_map/psum | solution.py:9
  327.9 3.4 copy.29
  331.3 1.4 copy.30
  (65 shorter events, 13.4 us)
Async XLA Ops:
  7.2 146.1 %all-reduce.5.cloned.1.call-start = ((), (), s32[]{:S(2)}) async-start(), calls=%async_computation | async-start | bytes 9437184 | tf_op jit(solution)/shard_map/psum | solution.py:9
  8.0 5.2 %collective-permute-start = (bf16[1,96,256]{2,1,0:T(8,128)(2,1)S(1)}, bf16[1,96,256]{2,1,0:T(8,128)(2,1)S(1)}, u32[]{:S(2)}, u32[]{:S(2)}) collective-permute-start(bf16[1,96,256]{2,1,0:T(8,128)(2,1)S(1)} %get-tuple-element.58), channel_id=1, source_target_pairs={{0,4},{4,8},{8,12},{12,16},{16,20},{20,24},{24,28},{28,0},{1,5},{5... | collective-permute-start | bytes 147464 | tf_op jit(solution)/shard_map/ppermute | solution.py:19
  8.6 5.8 %collective-permute-start.1 = (bf16[1,96,256]{2,1,0:T(8,128)(2,1)S(1)}, bf16[1,96,256]{2,1,0:T(8,128)(2,1)S(1)}, u32[]{:S(2)}, u32[]{:S(2)}) collective-permute-start(bf16[1,96,256]{2,1,0:T(8,128)(2,1)S(1)} %get-tuple-element.57), channel_id=1, source_target_pairs={{4,0},{8,4},{12,8},{16,12},{20,16},{24,20},{28,24},{0,28},{5,1},{9... | collective-permute-start | bytes 147464 | tf_op jit(solution)/shard_map/ppermute | solution.py:22
  14.5 5.9 %collective-permute-start.3 = (bf16[18,1,256]{2,1,0:T(2,128)(2,1)S(1)}, bf16[18,1,256]{2,1,0:T(2,128)(2,1)S(1)}, u32[]{:S(2)}, u32[]{:S(2)}) collective-permute-start(bf16[18,1,256]{2,1,0:T(2,128)(2,1)S(1)} %get-tuple-element.50), channel_id=1, source_target_pairs={{1,0},{2,1},{3,2},{0,3},{5,4},{6,5},{7,6},{4,7},{9,8},{10,9},{11,1... | collective-permute-start | bytes 27656 | tf_op jit(solution)/shard_map/ppermute | solution.py:22
  18.9 5.6 %collective-permute-start.2 = (bf16[18,1,256]{2,1,0:T(2,128)(2,1)S(1)}, bf16[18,1,256]{2,1,0:T(2,128)(2,1)S(1)}, u32[]{:S(2)}, u32[]{:S(2)}) collective-permute-start(bf16[18,1,256]{2,1,0:T(2,128)(2,1)S(1)} %get-tuple-element.49), channel_id=1, source_target_pairs={{0,1},{1,2},{2,3},{3,0},{4,5},{5,6},{6,7},{7,4},{8,9},{9,10},{10,1... | collective-permute-start | bytes 27656 | tf_op jit(solution)/shard_map/ppermute | solution.py:19
  25.0 1.3 copy-start.1
  30.0 2.0 collective-permute-start.5
  30.0 4.5 %collective-permute-start.4 = (bf16[1,96,256]{2,1,0:T(8,128)(2,1)S(1)}, bf16[1,96,256]{2,1,0:T(8,128)(2,1)S(1)}, u32[]{:S(2)}, u32[]{:S(2)}) collective-permute-start(bf16[1,96,256]{2,1,0:T(8,128)(2,1)S(1)} %get-tuple-element.55), channel_id=1, source_target_pairs={{0,4},{4,8},{8,12},{12,16},{16,20},{20,24},{24,28},{28,0},{1,5},{5... | collective-permute-start | bytes 147464 | tf_op jit(solution)/shard_map/ppermute | solution.py:19
  34.5 3.8 %collective-permute-start.7 = (bf16[18,1,256]{2,1,0:T(2,128)(2,1)S(1)}, bf16[18,1,256]{2,1,0:T(2,128)(2,1)S(1)}, u32[]{:S(2)}, u32[]{:S(2)}) collective-permute-start(bf16[18,1,256]{2,1,0:T(2,128)(2,1)S(1)} %get-tuple-element.48), channel_id=1, source_target_pairs={{1,0},{2,1},{3,2},{0,3},{5,4},{6,5},{7,6},{4,7},{9,8},{10,9},{11,1... | collective-permute-start | bytes 27656 | tf_op jit(solution)/shard_map/ppermute | solution.py:22
  34.8 5.6 %collective-permute-start.6 = (bf16[18,1,256]{2,1,0:T(2,128)(2,1)S(1)}, bf16[18,1,256]{2,1,0:T(2,128)(2,1)S(1)}, u32[]{:S(2)}, u32[]{:S(2)}) collective-permute-start(bf16[18,1,256]{2,1,0:T(2,128)(2,1)S(1)} %get-tuple-element.47), channel_id=1, source_target_pairs={{0,1},{1,2},{2,3},{3,0},{4,5},{5,6},{6,7},{7,4},{8,9},{9,10},{10,1... | collective-permute-start | bytes 27656 | tf_op jit(solution)/shard_map/ppermute | solution.py:19
  40.9 1.3 copy-start
  45.1 1.1 copy-start.5
  47.4 3.6 %collective-permute-start.9 = (bf16[1,96,256]{2,1,0:T(8,128)(2,1)S(1)}, bf16[1,96,256]{2,1,0:T(8,128)(2,1)S(1)}, u32[]{:S(2)}, u32[]{:S(2)}) collective-permute-start(bf16[1,96,256]{2,1,0:T(8,128)(2,1)S(1)} %get-tuple-element.54), channel_id=1, source_target_pairs={{4,0},{8,4},{12,8},{16,12},{20,16},{24,20},{28,24},{0,28},{5,1},{9... | collective-permute-start | bytes 147464 | tf_op jit(solution)/shard_map/ppermute | solution.py:22
  47.5 4.6 %collective-permute-start.8 = (bf16[1,96,256]{2,1,0:T(8,128)(2,1)S(1)}, bf16[1,96,256]{2,1,0:T(8,128)(2,1)S(1)}, u32[]{:S(2)}, u32[]{:S(2)}) collective-permute-start(bf16[1,96,256]{2,1,0:T(8,128)(2,1)S(1)} %get-tuple-element.53), channel_id=1, source_target_pairs={{0,4},{4,8},{8,12},{12,16},{16,20},{20,24},{24,28},{28,0},{1,5},{5... | collective-permute-start | bytes 147464 | tf_op jit(solution)/shard_map/ppermute | solution.py:19
  52.2 3.8 %collective-permute-start.11 = (bf16[18,1,256]{2,1,0:T(2,128)(2,1)S(1)}, bf16[18,1,256]{2,1,0:T(2,128)(2,1)S(1)}, u32[]{:S(2)}, u32[]{:S(2)}) collective-permute-start(bf16[18,1,256]{2,1,0:T(2,128)(2,1)S(1)} %get-tuple-element.46), channel_id=1, source_target_pairs={{1,0},{2,1},{3,2},{0,3},{5,4},{6,5},{7,6},{4,7},{9,8},{10,9},{11,1... | collective-permute-start | bytes 27656 | tf_op jit(solution)/shard_map/ppermute | solution.py:22
  52.2 5.6 %collective-permute-start.10 = (bf16[18,1,256]{2,1,0:T(2,128)(2,1)S(1)}, bf16[18,1,256]{2,1,0:T(2,128)(2,1)S(1)}, u32[]{:S(2)}, u32[]{:S(2)}) collective-permute-start(bf16[18,1,256]{2,1,0:T(2,128)(2,1)S(1)} %get-tuple-element.45), channel_id=1, source_target_pairs={{0,1},{1,2},{2,3},{3,0},{4,5},{5,6},{6,7},{7,4},{8,9},{9,10},{10,1... | collective-permute-start | bytes 27656 | tf_op jit(solution)/shard_map/ppermute | solution.py:19
  54.7 4.8 %copy-start.3 = (f32[9,256,256]{2,1,0:T(8,128)}, f32[9,256,256]{2,1,0:T(8,128)S(1)}, u32[]{:S(2)}) copy-start(f32[9,256,256]{2,1,0:T(8,128)S(1)} %fusion.13) | copy-start | bytes 7077892
  67.6 1.4 copy-start.4
  69.0 258.9 %all-reduce.7.cloned.1.call-start = ((), (), s32[]{:S(2)}) async-start(), calls=%async_computation.1 | async-start | bytes 9437184 | tf_op jit(solution)/shard_map/psum | solution.py:9
  153.3 3.0 collective-permute-start.13
  154.3 4.4 %collective-permute-start.12 = (bf16[1,96,256]{2,1,0:T(8,128)(2,1)S(1)}, bf16[1,96,256]{2,1,0:T(8,128)(2,1)S(1)}, u32[]{:S(2)}, u32[]{:S(2)}) collective-permute-start(bf16[1,96,256]{2,1,0:T(8,128)(2,1)S(1)} %get-tuple-element.51), channel_id=1, source_target_pairs={{0,4},{4,8},{8,12},{12,16},{16,20},{20,24},{24,28},{28,0},{1,5},{5... | collective-permute-start | bytes 147464 | tf_op jit(solution)/shard_map/ppermute | solution.py:19
  158.7 5.2 %collective-permute-start.15 = (bf16[18,1,256]{2,1,0:T(2,128)(2,1)S(1)}, bf16[18,1,256]{2,1,0:T(2,128)(2,1)S(1)}, u32[]{:S(2)}, u32[]{:S(2)}) collective-permute-start(bf16[18,1,256]{2,1,0:T(2,128)(2,1)S(1)} %get-tuple-element.44), channel_id=1, source_target_pairs={{1,0},{2,1},{3,2},{0,3},{5,4},{6,5},{7,6},{4,7},{9,8},{10,9},{11,1... | collective-permute-start | bytes 27656 | tf_op jit(solution)/shard_map/ppermute | solution.py:22
  162.1 6.1 %collective-permute-start.14 = (bf16[18,1,256]{2,1,0:T(2,128)(2,1)S(1)}, bf16[18,1,256]{2,1,0:T(2,128)(2,1)S(1)}, u32[]{:S(2)}, u32[]{:S(2)}) collective-permute-start(bf16[18,1,256]{2,1,0:T(2,128)(2,1)S(1)} %get-tuple-element.43), channel_id=1, source_target_pairs={{0,1},{1,2},{2,3},{3,0},{4,5},{5,6},{6,7},{7,4},{8,9},{9,10},{10,1... | collective-permute-start | bytes 27656 | tf_op jit(solution)/shard_map/ppermute | solution.py:19
  327.9 3.4 copy-start.2
Sparse Core Ops, SparseCore 0:
  69.1 84.0 all-reduce.4
  155.7 172.1 all-reduce.6
